TPU v7x, 32 devices: a whole 2x2x4 slice. The times are simulated.
32 devices in a mesh: rows: 16 (over z, y, x), feat: 2 (over core).
Axes of the slice: x: 2, y: 2, z: 4, core: 2. Of those that a mesh axis runs over, the one named last changes fastest.
Arguments:
- queries: bfloat16 [1024, 128], P('rows', 'feat'), may hold values from -6 to 6
- corpus: bfloat16 [524288, 128], P(('rows', 'feat')), as said below
- candidates: int32 [1024, 100], P(('rows', 'feat')), may hold values from 0 to 524287, as said below
- threshold: int32 [1024], replicated, may hold values from 100 to 199, as said below
Outputs:
- exceed: float32 [1024], P(('rows', 'feat'))
- candidate_scores: float32 [1024, 100], P(('rows', 'feat'))
Inputs may be any that keep to these rules, and one draw needn't show every extreme that they name: Passage ids. Of the 3200 candidates of one device's queries (aligned blocks of 32 rows), at most 100 lie in the 16384 passages of any one device, and exactly 100 in some device's. `corpus`: passage embeddings of order one or smaller; their scale differs between passages. Some query has threshold 100 and some 199.
All inputs are finite; a program needn't handle non-finite values.
Results may differ from a plain program's by a relative error of at most 0.00035.
Values may be sent and summed in bfloat16 or wider, within the bound.
A program may use at most 64 MiB of HBM per device.

v0:
```python
import jax
import jax.numpy as jnp
from jax import lax
from jax.sharding import PartitionSpec as P


def body(queries, corpus, candidates, threshold):
    rows_dev = corpus.shape[0]
    width = corpus.shape[1]
    shards = lax.axis_size("rows") * lax.axis_size("feat")
    owned_queries = candidates.shape[0]
    per_query = candidates.shape[1]
    npass_all = rows_dev * shards
    cutoff = threshold.astype(jnp.float32) * 0.01
    owner = lax.axis_index(("rows", "feat"))
    full_rows = lax.all_gather(queries, "feat", axis=1, tiled=True)
    whole = lax.all_gather(full_rows, "rows", axis=0, tiled=True)
    query_count = whole.shape[0]
    block = 2048
    corpus_blocks = corpus.reshape(rows_dev // block, block, width)

    def visit(total, block_rows):
        scores = lax.dot_general(
            whole, block_rows, (((1,), (1,)), ((), ())), preferred_element_type=jnp.float32
        )
        return (total + jnp.sum(jnp.maximum(scores - cutoff[:, None], 0.0), axis=1), None)

    total, _ = lax.scan(visit, jnp.zeros((query_count,), jnp.float32), corpus_blocks)
    flat_ids = candidates.reshape(-1)
    total_ids = flat_ids.shape[0]
    capacity = (total_ids + shards - 1) // shards
    target = flat_ids // rows_dev
    onehot = (target[:, None] == jnp.arange(shards, dtype=jnp.int32)[None, :]).astype(jnp.int32)
    before = jnp.cumsum(onehot, axis=0) - onehot
    rank = jnp.sum(before * onehot, axis=1)
    query_ids = owner * owned_queries + jnp.arange(total_ids, dtype=jnp.int32) // per_query
    fields = jnp.stack([flat_ids - target * rows_dev, query_ids], axis=1)
    send_both = jnp.zeros((shards, capacity, 2), jnp.int32).at[target, rank].set(fields)
    n_rows = lax.axis_size("rows")
    n_feat = lax.axis_size("feat")
    received = lax.all_to_all(
        lax.all_to_all(
            send_both.reshape(n_rows, n_feat, capacity * 2),
            "rows",
            split_axis=0,
            concat_axis=0,
            tiled=True,
        ),
        "feat",
        split_axis=1,
        concat_axis=1,
        tiled=True,
    )
    received = received.reshape(shards * capacity, 2)
    picked = corpus[received[:, 0]]
    asked = whole[received[:, 1]]
    values = jnp.einsum("kd,kd->k", picked, asked, preferred_element_type=jnp.float32).reshape(
        n_rows, n_feat, capacity
    )
    partials = total.reshape(n_rows, n_feat, owned_queries)
    answers, mass_parts = (
        lax.all_to_all(
            lax.all_to_all(values, "rows", split_axis=0, concat_axis=0, tiled=True),
            "feat",
            split_axis=1,
            concat_axis=1,
            tiled=True,
        ),
        lax.all_to_all(
            lax.all_to_all(partials, "rows", split_axis=0, concat_axis=0, tiled=True),
            "feat",
            split_axis=1,
            concat_axis=1,
            tiled=True,
        ),
    )
    exceed = jnp.sum(mass_parts, axis=(0, 1)) * (8.0 / npass_all)
    candidate_scores = answers.reshape(shards, capacity)[target, rank].reshape(
        owned_queries, per_query
    )
    return (exceed, candidate_scores)


def solution(mesh):
    return jax.shard_map(
        body,
        mesh=mesh,
        in_specs=(P("rows", "feat"), P(("rows", "feat"), None), P(("rows", "feat"), None), P()),
        out_specs=(P(("rows", "feat")), P(("rows", "feat"), None)),
        check_vma=False,
    )
```

profile of v0, /device:TPU:0, one launch (start us, length us, event | category | flops | bytes accessed | tf_op | source)
XLA Modules:
  0.0 177.3 jit_solution(1144586767254924828)
XLA Ops:
  1.4 2.0 %all_gather.6 = bf16[64,128]{0,1:T(8,128)(2,1)S(1)} all-gather(bf16[64,64]{0,1:T(8,128)(2,1)S(1)} %copy.40), channel_id=1, replica_groups=mesh['rows'=16,'feat'=2] {'feat'}, dimensions={1}, use_global_device_ids=true | all-gather | bytes 24576 | tf_op jit(solution)/shard_map/all_gather | solution.py:16
  3.5 43.7 %all_gather.7 = bf16[1024,128]{1,0:T(8,128)(2,1)S(1)} all-gather(bf16[64,128]{1,0:T(8,128)(2,1)S(1)} %copy.41), channel_id=1, replica_groups=mesh['rows'=16,'feat'=2] {'rows'}, dimensions={0}, use_global_device_ids=true | all-gather | bytes 278528 | tf_op jit(solution)/shard_map/all_gather | solution.py:17
  47.9 18.8 %while.11 = (s32[]{:T(128)}, f32[1024]{0:T(1024)S(1)}, bf16[8,2048,128]{2,1,0:T(8,128)(2,1)}, bf16[1024,128]{1,0:T(8,128)(2,1)S(1)}, f32[1024]{0:T(1024)S(1)}, /*index=5*/s32[]{:T(128)}, s32[]{:T(128)}) while((s32[]{:T(128)}, f32[1024]{0:T(1024)S(1)}, bf16[8,2048,128]{2,1,0:T(8,128)(2,1)}, bf16[1024,128]{1,0:T(8,128)(2,1)S(1)}, ...), condition=%wide.region_2.3_spmd.clone, body=%wide.region_0.2_spmd.clone.sunk | while | flops 543163392 | bytes 807511 | solution.py:28
  47.9 2.3 %maximum_reduce_fusion.2 = f32[1024]{0:T(1024)S(1)} fusion(bf16[1024,128]{1,0:T(8,128)(2,1)S(1)} %get-tuple-element.115, f32[1024]{0:T(1024)S(1)} %get-tuple-element.116, bf16[8,2048,128]{2,1,0:T(8,128)(2,1)} %get-tuple-element.114, s32[]{:T(128)} %get-tuple-element.105), kind=kOutput, calls=%fused_computation.4.clone.1 | convolution fusion | flops 543161344 | bytes 795136 | tf_op jit(solution)/shard_map/while/body/eval_jaxpr/dot_general | solution.py:23
  50.2 2.3 %maximum_reduce_fusion.2 = f32[1024]{0:T(1024)S(1)} fusion(bf16[1024,128]{1,0:T(8,128)(2,1)S(1)} %get-tuple-element.115, f32[1024]{0:T(1024)S(1)} %get-tuple-element.116, bf16[8,2048,128]{2,1,0:T(8,128)(2,1)} %get-tuple-element.114, s32[]{:T(128)} %get-tuple-element.105), kind=kOutput, calls=%fused_computation.4.clone.1 | convolution fusion | flops 543161344 | bytes 795136 | tf_op jit(solution)/shard_map/while/body/eval_jaxpr/dot_general | solution.py:23
  52.6 2.3 %maximum_reduce_fusion.2 = f32[1024]{0:T(1024)S(1)} fusion(bf16[1024,128]{1,0:T(8,128)(2,1)S(1)} %get-tuple-element.115, f32[1024]{0:T(1024)S(1)} %get-tuple-element.116, bf16[8,2048,128]{2,1,0:T(8,128)(2,1)} %get-tuple-element.114, s32[]{:T(128)} %get-tuple-element.105), kind=kOutput, calls=%fused_computation.4.clone.1 | convolution fusion | flops 543161344 | bytes 795136 | tf_op jit(solution)/shard_map/while/body/eval_jaxpr/dot_general | solution.py:23
  54.9 2.3 %maximum_reduce_fusion.2 = f32[1024]{0:T(1024)S(1)} fusion(bf16[1024,128]{1,0:T(8,128)(2,1)S(1)} %get-tuple-element.115, f32[1024]{0:T(1024)S(1)} %get-tuple-element.116, bf16[8,2048,128]{2,1,0:T(8,128)(2,1)} %get-tuple-element.114, s32[]{:T(128)} %get-tuple-element.105), kind=kOutput, calls=%fused_computation.4.clone.1 | convolution fusion | flops 543161344 | bytes 795136 | tf_op jit(solution)/shard_map/while/body/eval_jaxpr/dot_general | solution.py:23
  57.3 2.3 %maximum_reduce_fusion.2 = f32[1024]{0:T(1024)S(1)} fusion(bf16[1024,128]{1,0:T(8,128)(2,1)S(1)} %get-tuple-element.115, f32[1024]{0:T(1024)S(1)} %get-tuple-element.116, bf16[8,2048,128]{2,1,0:T(8,128)(2,1)} %get-tuple-element.114, s32[]{:T(128)} %get-tuple-element.105), kind=kOutput, calls=%fused_computation.4.clone.1 | convolution fusion | flops 543161344 | bytes 795136 | tf_op jit(solution)/shard_map/while/body/eval_jaxpr/dot_general | solution.py:23
  59.6 2.3 %maximum_reduce_fusion.2 = f32[1024]{0:T(1024)S(1)} fusion(bf16[1024,128]{1,0:T(8,128)(2,1)S(1)} %get-tuple-element.115, f32[1024]{0:T(1024)S(1)} %get-tuple-element.116, bf16[8,2048,128]{2,1,0:T(8,128)(2,1)} %get-tuple-element.114, s32[]{:T(128)} %get-tuple-element.105), kind=kOutput, calls=%fused_computation.4.clone.1 | convolution fusion | flops 543161344 | bytes 795136 | tf_op jit(solution)/shard_map/while/body/eval_jaxpr/dot_general | solution.py:23
  62.0 2.3 %maximum_reduce_fusion.2 = f32[1024]{0:T(1024)S(1)} fusion(bf16[1024,128]{1,0:T(8,128)(2,1)S(1)} %get-tuple-element.115, f32[1024]{0:T(1024)S(1)} %get-tuple-element.116, bf16[8,2048,128]{2,1,0:T(8,128)(2,1)} %get-tuple-element.114, s32[]{:T(128)} %get-tuple-element.105), kind=kOutput, calls=%fused_computation.4.clone.1 | convolution fusion | flops 543161344 | bytes 795136 | tf_op jit(solution)/shard_map/while/body/eval_jaxpr/dot_general | solution.py:23
  64.3 2.3 %maximum_reduce_fusion.2 = f32[1024]{0:T(1024)S(1)} fusion(bf16[1024,128]{1,0:T(8,128)(2,1)S(1)} %get-tuple-element.115, f32[1024]{0:T(1024)S(1)} %get-tuple-element.116, bf16[8,2048,128]{2,1,0:T(8,128)(2,1)} %get-tuple-element.114, s32[]{:T(128)} %get-tuple-element.105), kind=kOutput, calls=%fused_computation.4.clone.1 | convolution fusion | flops 543161344 | bytes 795136 | tf_op jit(solution)/shard_map/while/body/eval_jaxpr/dot_general | solution.py:23
  67.3 4.1 %all-to-all-start = ((f32[16,2,32]{2,1,0:T(2,128)}), f32[16,2,32]{2,1,0:T(2,128)}, u32[]{:S(2)}, u32[]{:S(2)}) async-start(f32[16,2,32]{2,1,0:T(2,128)} %reshape.217), calls=%async_computation | async-start | bytes 32768 | tf_op jit(solution)/shard_map/all_to_all | solution.py:70
  71.9 9.2 %reduce-window.6 = s32[32,25,128]{2,1,0:T(8,128)S(1)} reduce-window(s32[32,25,128]{2,1,0:T(8,128)S(1)} %fusion.6, s32[]{:T(128)} %constant.28.clone.1), window={size=1x1x128 pad=0_0x0_0x127_0}, to_apply=%region_4.5 | reduce-window | flops 13004800 | bytes 819204 | tf_op jit(solution)/shard_map/reduce-window
  84.2 13.8 %scatter_custom_fusion = s32[3200,2]{1,0:T(8,128)S(1)} fusion(s32[3200]{0:T(1024)} %broadcast_select_fusion, s32[3200,2]{1,0:T(8,128)S(1)} %copy.44, s32[]{:T(128)} %constant.28.clone.1), kind=kCustom, calls=%fused_computation.11 | custom fusion | bytes 26112
  100.2 3.7 %all_to_all.30 = f32[2,1,512]{2,1,0:T(1,128)S(1)} all-to-all(f32[2,1,512]{2,1,0:T(1,128)S(1)} %reshape.269), channel_id=1, replica_groups=mesh['rows'=16,'feat'=2] {'feat'}, dimensions={0} | all-to-all | bytes 8192 | tf_op jit(solution)/shard_map/all_to_all | solution.py:69
  103.8 6.8 %all-to-all-start.2 = ((s32[16,2,200]{2,1,0:T(2,128)}), s32[16,2,200]{2,1,0:T(2,128)S(1)}, u32[]{:S(2)}, u32[]{:S(2)}) async-start(s32[16,2,200]{2,1,0:T(2,128)} %reshape.222), calls=%async_computation.2 | async-start | bytes 65536 | tf_op jit(solution)/shard_map/all_to_all | solution.py:42
  112.5 5.6 %all-to-all-done.2 = s32[16,2,200]{2,1,0:T(2,128)S(1)} async-done(((s32[16,2,200]{2,1,0:T(2,128)}), s32[16,2,200]{2,1,0:T(2,128)S(1)}, u32[]{:S(2)}, u32[]{:S(2)}) %all-to-all-start.2) | async-done | bytes 25632 | tf_op jit(solution)/shard_map/all_to_all | solution.py:42
  118.1 3.7 %all_to_all.31 = s32[16,2,200]{2,0,1:T(8,128)S(1)} all-to-all(s32[16,2,200]{2,0,1:T(8,128)S(1)} %copy.45), channel_id=1, replica_groups=mesh['rows'=16,'feat'=2] {'feat'}, dimensions={1} | all-to-all | bytes 51200 | tf_op jit(solution)/shard_map/all_to_all | solution.py:41
  126.0 6.7 %gather_fusion.1 = bf16[3200,128]{1,0:T(8,128)(2,1)S(1)} fusion(bf16[1024,128]{1,0:T(8,128)(2,1)S(1)} %get-tuple-element.119, s32[4096]{0:T(1024)S(1)} %pad_clamp_fusion), kind=kCustom, calls=%fused_computation.1 | custom fusion | bytes 1651200 | tf_op jit(solution)/shard_map/gather | solution.py:56
  133.3 8.5 %gather_fusion = bf16[3200,128]{1,0:T(8,128)(2,1)S(1)} fusion(bf16[16384,128]{1,0:T(8,128)(2,1)} %bitcast.35, s32[4096]{0:T(1024)S(1)} %pad_clamp_fusion.1), kind=kCustom, calls=%fused_computation | custom fusion | bytes 1651200 | tf_op jit(solution)/shard_map/gather | solution.py:55
  143.1 3.5 %all-to-all-start.4 = ((f32[16,2,100]{2,1,0:T(2,128)}), f32[16,2,100]{2,1,0:T(2,128)S(1)}, u32[]{:S(2)}, u32[]{:S(2)}) async-start(f32[16,2,100]{2,1,0:T(2,128)} %reshape.224), calls=%async_computation.4 | async-start | bytes 32768 | tf_op jit(solution)/shard_map/all_to_all | solution.py:63
  147.1 6.8 %all-to-all-done.4 = f32[16,2,100]{2,1,0:T(2,128)S(1)} async-done(((f32[16,2,100]{2,1,0:T(2,128)}), f32[16,2,100]{2,1,0:T(2,128)S(1)}, u32[]{:S(2)}, u32[]{:S(2)}) %all-to-all-start.4) | async-done | bytes 12832 | tf_op jit(solution)/shard_map/all_to_all | solution.py:63
  153.9 3.7 %all_to_all.32 = f32[16,2,100]{2,0,1:T(8,128)S(1)} all-to-all(f32[16,2,100]{2,0,1:T(8,128)S(1)} %copy.49), channel_id=1, replica_groups=mesh['rows'=16,'feat'=2] {'feat'}, dimensions={1} | all-to-all | bytes 25600 | tf_op jit(solution)/shard_map/all_to_all | solution.py:62
  157.6 19.0 %gather_fusion.2 = f32[3200]{0:T(1024)S(1)} fusion(f32[32,100]{1,0:T(8,128)S(1)} %bitcast.33, s32[3200]{0:T(1024)S(1)} %get-tuple-element.58), kind=kCustom, calls=%fused_computation.2 | custom fusion | bytes 51200 | tf_op jit(solution)/shard_map/gather | solution.py:78
  (62 shorter events, 16.9 us)
Async XLA Ops:
  47.9 23.6 %copy-start = (s32[32,100]{1,0:T(8,128)S(1)}, s32[32,100]{1,0:T(8,128)}, u32[]{:S(2)}) copy-start(s32[32,100]{1,0:T(8,128)} %param.8) | copy-start | bytes 38404
  67.3 32.0 %all-to-all-start = ((f32[16,2,32]{2,1,0:T(2,128)}), f32[16,2,32]{2,1,0:T(2,128)}, u32[]{:S(2)}, u32[]{:S(2)}) async-start(f32[16,2,32]{2,1,0:T(2,128)} %reshape.217), calls=%async_computation | async-start | bytes 32768 | tf_op jit(solution)/shard_map/all_to_all | solution.py:70
  71.9 11.0 %copy-start.2 = (s32[2]{0:T(128)S(1)}, s32[2]{0:T(128)}, u32[]{:S(2)}) copy-start(s32[2]{0:T(128)} %constant.67) | copy-start | bytes 28
  71.9 11.1 %copy-start.1 = (s32[2]{0:T(128)S(1)}, s32[2]{0:T(128)}, u32[]{:S(2)}) copy-start(s32[2]{0:T(128)} %constant.64) | copy-start | bytes 28
  103.8 14.2 %all-to-all-start.2 = ((s32[16,2,200]{2,1,0:T(2,128)}), s32[16,2,200]{2,1,0:T(2,128)S(1)}, u32[]{:S(2)}, u32[]{:S(2)}) async-start(s32[16,2,200]{2,1,0:T(2,128)} %reshape.222), calls=%async_computation.2 | async-start | bytes 65536 | tf_op jit(solution)/shard_map/all_to_all | solution.py:42
  141.8 4.8 %copy-start.3 = (f32[32]{0:T(128)S(1)}, f32[32]{0:T(128)}, u32[]{:S(2)}) copy-start(f32[32]{0:T(128)} %bitcast_reduce_fusion) | copy-start | bytes 388
  143.1 10.8 %all-to-all-start.4 = ((f32[16,2,100]{2,1,0:T(2,128)}), f32[16,2,100]{2,1,0:T(2,128)S(1)}, u32[]{:S(2)}, u32[]{:S(2)}) async-start(f32[16,2,100]{2,1,0:T(2,128)} %reshape.224), calls=%async_computation.4 | async-start | bytes 32768 | tf_op jit(solution)/shard_map/all_to_all | solution.py:63
where the time goes:
time: 178 us; the launch traced here: 177 us
  local copies, waits for them, and re-layouts  59.9 us (34%)
  blocking collectives  56.8 us (32%)
  matrix products  18.5 us (10%)
  starting transfers between devices  14.4 us (8%)
  other arithmetic  14.1 us (8%)
  waiting for transfers between devices  12.4 us (7%)
    all_gather x1, blocking collectives, body(): whole = lax.all_gather(full_rows, 'rows', axis=0, tiled=True)  43.7 us
    gather x1, local copies, waits for them, and re-layouts, body(): answers.reshape(shards, capacity)[target, rank]  19 us
    dot_general x8, matrix products, visit(): lax.dot_general(whole, block_rows, (((1,), (1,)), ((), ())), preferred_el...  18.5 us
    unnamed x14, local copies, waits for them, and re-layouts  17.2 us
    another operation x3, other arithmetic  9.61 us
    gather x1, local copies, waits for them, and re-layouts, body(): picked = corpus[received[:, 0]]  8.49 us
    all_to_all x1, starting transfers between devices, body(): lax.all_to_all(send_both.reshape(n_rows, n_feat, capacity * 2), 'rows', s...  6.81 us
    all_to_all x1, waiting for transfers between devices, body(): lax.all_to_all(values, 'rows', split_axis=0, concat_axis=0, tiled=True)  6.78 us
  transfers between devices with their start and end apart: 3, of which 2 were waited for; matrix products, arithmetic and copies ran while one was open for 17% of the time, Pallas kernels for 0%

commit v1 on v0

--- a/solution.py
+++ b/solution.py
@@ -2,6 +2,28 @@
 import jax.numpy as jnp
 from jax import lax
 from jax.sharding import PartitionSpec as P
+
+
+def joined_along(blocks, dim):
+    blocks = jnp.moveaxis(blocks, 0, dim)
+    shape = blocks.shape
+    return blocks.reshape(*shape[:dim], shape[dim] * shape[dim + 1], *shape[dim + 2 :])
+
+
+def doubled(x, axis):
+    size = lax.axis_size(axis)
+    pieces = x[None]
+    for level in range(size.bit_length() - 1):
+        distance = 1 << level
+        theirs = lax.ppermute(pieces, axis, [(i, i ^ distance) for i in range(size)])
+        both = jnp.stack([pieces, theirs])
+        upper = lax.axis_index(axis) >> level & 1
+        pieces = jnp.where(upper == 0, both, both[::-1]).reshape(-1, *x.shape)
+    return pieces
+
+
+def doubled_up(x, axis, dim):
+    return joined_along(doubled(x, axis), dim)
 
 
 def body(queries, corpus, candidates, threshold):
@@ -14,7 +36,7 @@
     cutoff = threshold.astype(jnp.float32) * 0.01
     owner = lax.axis_index(("rows", "feat"))
     full_rows = lax.all_gather(queries, "feat", axis=1, tiled=True)
-    whole = lax.all_gather(full_rows, "rows", axis=0, tiled=True)
+    whole = doubled_up(full_rows, "rows", 0)
     query_count = whole.shape[0]
     block = 2048
     corpus_blocks = corpus.reshape(rows_dev // block, block, width)

time: 178 us -> 149 us (0.84)
  blocking collectives: 56.8 us -> 13.1 us
  waiting for transfers between devices: 12.4 us -> 21.8 us
  starting transfers between devices: 14.4 us -> 19.5 us
    all_gather x1 -> x0, blocking collectives: 43.7 us -> none  [body(): whole = lax.all_gather(full_rows, 'rows', axis=0, tiled=True)]
    ppermute x0 -> x4, starting transfers between devices: none -> 6.25 us  [doubled(): lax.ppermute(pieces, axis, [(i, i ^ distance) for i in range(size)])]
    all_to_all x1, waiting for transfers between devices: 0.01 us -> 6.11 us  [body(): lax.all_to_all(partials, 'rows', split_axis=0, concat_axis=0, tiled=True)]
    ppermute x0 -> x4, waiting for transfers between devices: none -> 4.92 us  [doubled(): lax.ppermute(pieces, axis, [(i, i ^ distance) for i in range(size)])]
    reshape x3, local copies, waits for them, and re-layouts: 0.31 us -> 2.46 us  [body(): flat_ids = candidates.reshape(-1)]
    another operation x3 -> x8, other arithmetic: 9.61 us -> 9.79 us
    unnamed x14 -> x12, local copies, waits for them, and re-layouts: 17.2 us -> 17 us
  transfers between devices with their start and end apart: 3 -> 7, of which waited for: 2 -> 4; matrix products, arithmetic and copies ran while one was open for 17% -> 31% of each run, Pallas kernels for 0% -> 0%
where the time goes in v1:
time: 149 us; the launch traced here: 148 us
  local copies, waits for them, and re-layouts  61.3 us (41%)
  waiting for transfers between devices  21.8 us (15%)
  starting transfers between devices  19.5 us (13%)
  matrix products  18.4 us (12%)
  blocking collectives  13.1 us (9%)
  other arithmetic  12.7 us (9%)
    gather x1, local copies, waits for them, and re-layouts, body(): answers.reshape(shards, capacity)[target, rank]  19 us
    dot_general x8, matrix products, visit(): lax.dot_general(whole, block_rows, (((1,), (1,)), ((), ())), preferred_el...  18.4 us
    unnamed x12, local copies, waits for them, and re-layouts  17 us
    another operation x3, other arithmetic  9.61 us
    gather x1, local copies, waits for them, and re-layouts, body(): picked = corpus[received[:, 0]]  8.48 us
    gather x1, local copies, waits for them, and re-layouts, body(): asked = whole[received[:, 1]]  6.72 us
    ppermute x4, starting transfers between devices, doubled(): lax.ppermute(pieces, axis, [(i, i ^ distance) for i in range(size)])  6.25 us
    all_to_all x1, waiting for transfers between devices, body(): lax.all_to_all(partials, 'rows', split_axis=0, concat_axis=0, tiled=True)  6.11 us
  transfers between devices with their start and end apart: 7, of which 4 were waited for; matrix products, arithmetic and copies ran while one was open for 31% of the time, Pallas kernels for 0%

profile of v1, /device:TPU:0, one launch (start us, length us, event | category | flops | bytes accessed | tf_op | source)
XLA Modules:
  0.0 148.1 jit_solution(15506852797543582765)
XLA Ops:
  3.4 2.9 %collective-permute-start = (bf16[1,64,128]{1,2,0:T(8,128)(2,1)S(1)}, bf16[1,64,128]{1,2,0:T(8,128)(2,1)S(1)}, u32[]{:S(2)}, u32[]{:S(2)}) collective-permute-start(bf16[1,64,128]{1,2,0:T(8,128)(2,1)S(1)} %bitcast.57), channel_id=1, source_target_pairs={{0,2},{2,0},{4,6},{6,4},{8,10},{10,8},{12,14},{14,12},{16,18},{18,... | collective-permute-start | bytes 49160 | tf_op jit(solution)/shard_map/ppermute | solution.py:18
  8.9 9.2 %reduce-window.6 = s32[32,25,128]{2,1,0:T(8,128)S(1)} reduce-window(s32[32,25,128]{2,1,0:T(8,128)S(1)} %fusion.6, s32[]{:T(128)} %constant.23.clone.1), window={size=1x1x128 pad=0_0x0_0x127_0}, to_apply=%region_4.5 | reduce-window | flops 13004800 | bytes 819204 | tf_op jit(solution)/shard_map/reduce-window
  20.6 13.7 %scatter_custom_fusion = s32[3200,2]{1,0:T(8,128)S(1)} fusion(s32[3200]{0:T(1024)S(1)} %broadcast_select_fusion, s32[3200,2]{1,0:T(8,128)S(1)} %copy.47, s32[]{:T(128)} %constant.23.clone.1), kind=kCustom, calls=%fused_computation.11 | custom fusion | bytes 25604
  35.6 5.9 %all-to-all-start.2 = ((s32[16,2,200]{2,1,0:T(2,128)}), s32[16,2,200]{2,1,0:T(2,128)S(1)}, u32[]{:S(2)}, u32[]{:S(2)}) async-start(s32[16,2,200]{2,1,0:T(2,128)} %reshape.234), calls=%async_computation.2 | async-start | bytes 65536 | tf_op jit(solution)/shard_map/all_to_all | solution.py:64
  43.7 5.3 %all-to-all-done.2 = s32[16,2,200]{2,1,0:T(2,128)S(1)} async-done(((s32[16,2,200]{2,1,0:T(2,128)}), s32[16,2,200]{2,1,0:T(2,128)S(1)}, u32[]{:S(2)}, u32[]{:S(2)}) %all-to-all-start.2) | async-done | bytes 25632 | tf_op jit(solution)/shard_map/all_to_all | solution.py:64
  49.0 3.7 %all_to_all.30 = s32[16,2,200]{2,0,1:T(8,128)S(1)} all-to-all(s32[16,2,200]{2,0,1:T(8,128)S(1)} %copy.48), channel_id=1, replica_groups=mesh['rows'=16,'feat'=2] {'feat'}, dimensions={1} | all-to-all | bytes 51200 | tf_op jit(solution)/shard_map/all_to_all | solution.py:63
  58.2 4.9 %collective-permute-done.2 = bf16[4,64,128]{1,2,0:T(8,128)(2,1)S(1)} collective-permute-done((bf16[4,64,128]{1,2,0:T(8,128)(2,1)S(1)}, bf16[4,64,128]{1,2,0:T(8,128)(2,1)S(1)}, u32[]{:S(2)}, u32[]{:S(2)}) %collective-permute-start.2) | collective-permute-done | bytes 65568 | tf_op jit(solution)/shard_map/ppermute | solution.py:18
  64.1 8.5 %gather_fusion = bf16[3200,128]{1,0:T(8,128)(2,1)S(1)} fusion(bf16[16384,128]{1,0:T(8,128)(2,1)} %param.7, s32[4096]{0:T(1024)S(1)} %pad_clamp_fusion.1), kind=kCustom, calls=%fused_computation | custom fusion | bytes 1651200 | tf_op jit(solution)/shard_map/gather | solution.py:77
  72.7 6.7 %gather_fusion.1 = bf16[3200,128]{1,0:T(8,128)(2,1)S(1)} fusion(bf16[1024,128]{1,0:T(8,128)(2,1)S(1)} %bitcast.49, s32[4096]{0:T(1024)S(1)} %pad_clamp_fusion), kind=kCustom, calls=%fused_computation.1 | custom fusion | bytes 1651200 | tf_op jit(solution)/shard_map/gather | solution.py:78
  79.5 18.8 %while.11 = (s32[]{:T(128)}, f32[1024]{0:T(1024)S(1)}, bf16[8,2048,128]{2,1,0:T(8,128)(2,1)}, bf16[1024,128]{1,0:T(8,128)(2,1)S(1)}, f32[1024]{0:T(1024)S(1)}, /*index=5*/s32[]{:T(128)}, s32[]{:T(128)}) while((s32[]{:T(128)}, f32[1024]{0:T(1024)S(1)}, bf16[8,2048,128]{2,1,0:T(8,128)(2,1)}, bf16[1024,128]{1,0:T(8,128)(2,1)S(1)}, ...), condition=%wide.region_2.3_spmd.clone, body=%wide.region_0.2_spmd.clone.sunk | while | flops 543163392 | bytes 807511 | solution.py:50
  79.5 2.3 %maximum_reduce_fusion.2 = f32[1024]{0:T(1024)S(1)} fusion(bf16[1024,128]{1,0:T(8,128)(2,1)S(1)} %get-tuple-element.117, f32[1024]{0:T(1024)S(1)} %get-tuple-element.118, bf16[8,2048,128]{2,1,0:T(8,128)(2,1)} %get-tuple-element.116, s32[]{:T(128)} %get-tuple-element.107), kind=kOutput, calls=%fused_computation.4.clone.1 | convolution fusion | flops 543161344 | bytes 795136 | tf_op jit(solution)/shard_map/while/body/eval_jaxpr/dot_general | solution.py:45
  81.8 2.3 %maximum_reduce_fusion.2 = f32[1024]{0:T(1024)S(1)} fusion(bf16[1024,128]{1,0:T(8,128)(2,1)S(1)} %get-tuple-element.117, f32[1024]{0:T(1024)S(1)} %get-tuple-element.118, bf16[8,2048,128]{2,1,0:T(8,128)(2,1)} %get-tuple-element.116, s32[]{:T(128)} %get-tuple-element.107), kind=kOutput, calls=%fused_computation.4.clone.1 | convolution fusion | flops 543161344 | bytes 795136 | tf_op jit(solution)/shard_map/while/body/eval_jaxpr/dot_general | solution.py:45
  84.2 2.3 %maximum_reduce_fusion.2 = f32[1024]{0:T(1024)S(1)} fusion(bf16[1024,128]{1,0:T(8,128)(2,1)S(1)} %get-tuple-element.117, f32[1024]{0:T(1024)S(1)} %get-tuple-element.118, bf16[8,2048,128]{2,1,0:T(8,128)(2,1)} %get-tuple-element.116, s32[]{:T(128)} %get-tuple-element.107), kind=kOutput, calls=%fused_computation.4.clone.1 | convolution fusion | flops 543161344 | bytes 795136 | tf_op jit(solution)/shard_map/while/body/eval_jaxpr/dot_general | solution.py:45
  86.5 2.3 %maximum_reduce_fusion.2 = f32[1024]{0:T(1024)S(1)} fusion(bf16[1024,128]{1,0:T(8,128)(2,1)S(1)} %get-tuple-element.117, f32[1024]{0:T(1024)S(1)} %get-tuple-element.118, bf16[8,2048,128]{2,1,0:T(8,128)(2,1)} %get-tuple-element.116, s32[]{:T(128)} %get-tuple-element.107), kind=kOutput, calls=%fused_computation.4.clone.1 | convolution fusion | flops 543161344 | bytes 795136 | tf_op jit(solution)/shard_map/while/body/eval_jaxpr/dot_general | solution.py:45
  88.9 2.3 %maximum_reduce_fusion.2 = f32[1024]{0:T(1024)S(1)} fusion(bf16[1024,128]{1,0:T(8,128)(2,1)S(1)} %get-tuple-element.117, f32[1024]{0:T(1024)S(1)} %get-tuple-element.118, bf16[8,2048,128]{2,1,0:T(8,128)(2,1)} %get-tuple-element.116, s32[]{:T(128)} %get-tuple-element.107), kind=kOutput, calls=%fused_computation.4.clone.1 | convolution fusion | flops 543161344 | bytes 795136 | tf_op jit(solution)/shard_map/while/body/eval_jaxpr/dot_general | solution.py:45
  91.2 2.3 %maximum_reduce_fusion.2 = f32[1024]{0:T(1024)S(1)} fusion(bf16[1024,128]{1,0:T(8,128)(2,1)S(1)} %get-tuple-element.117, f32[1024]{0:T(1024)S(1)} %get-tuple-element.118, bf16[8,2048,128]{2,1,0:T(8,128)(2,1)} %get-tuple-element.116, s32[]{:T(128)} %get-tuple-element.107), kind=kOutput, calls=%fused_computation.4.clone.1 | convolution fusion | flops 543161344 | bytes 795136 | tf_op jit(solution)/shard_map/while/body/eval_jaxpr/dot_general | solution.py:45
  95.9 2.3 %maximum_reduce_fusion.2 = f32[1024]{0:T(1024)S(1)} fusion(bf16[1024,128]{1,0:T(8,128)(2,1)S(1)} %get-tuple-element.117, f32[1024]{0:T(1024)S(1)} %get-tuple-element.118, bf16[8,2048,128]{2,1,0:T(8,128)(2,1)} %get-tuple-element.116, s32[]{:T(128)} %get-tuple-element.107), kind=kOutput, calls=%fused_computation.4.clone.1 | convolution fusion | flops 543161344 | bytes 795136 | tf_op jit(solution)/shard_map/while/body/eval_jaxpr/dot_general | solution.py:45
  98.9 3.8 %all-to-all-start = ((f32[16,2,32]{2,1,0:T(2,128)}), f32[16,2,32]{2,1,0:T(2,128)S(1)}, u32[]{:S(2)}, u32[]{:S(2)}) async-start(f32[16,2,32]{2,1,0:T(2,128)} %reshape.229), calls=%async_computation | async-start | bytes 32768 | tf_op jit(solution)/shard_map/all_to_all | solution.py:92
  104.0 6.1 %all-to-all-done = f32[16,2,32]{2,1,0:T(2,128)S(1)} async-done(((f32[16,2,32]{2,1,0:T(2,128)}), f32[16,2,32]{2,1,0:T(2,128)S(1)}, u32[]{:S(2)}, u32[]{:S(2)}) %all-to-all-start) | async-done | bytes 4128 | tf_op jit(solution)/shard_map/all_to_all | solution.py:92
  110.2 3.7 %all_to_all.31 = f32[2,1,512]{2,1,0:T(1,128)S(1)} all-to-all(f32[2,1,512]{2,1,0:T(1,128)S(1)} %reshape.281), channel_id=1, replica_groups=mesh['rows'=16,'feat'=2] {'feat'}, dimensions={0} | all-to-all | bytes 8192 | tf_op jit(solution)/shard_map/all_to_all | solution.py:91
  113.8 3.5 %all-to-all-start.4 = ((f32[16,2,100]{2,1,0:T(2,128)}), f32[16,2,100]{2,1,0:T(2,128)S(1)}, u32[]{:S(2)}, u32[]{:S(2)}) async-start(f32[16,2,100]{2,1,0:T(2,128)} %reshape.236), calls=%async_computation.4 | async-start | bytes 32768 | tf_op jit(solution)/shard_map/all_to_all | solution.py:85
  119.1 5.5 %all-to-all-done.4 = f32[16,2,100]{2,1,0:T(2,128)S(1)} async-done(((f32[16,2,100]{2,1,0:T(2,128)}), f32[16,2,100]{2,1,0:T(2,128)S(1)}, u32[]{:S(2)}, u32[]{:S(2)}) %all-to-all-start.4) | async-done | bytes 12832 | tf_op jit(solution)/shard_map/all_to_all | solution.py:85
  124.7 3.7 %all_to_all.32 = f32[16,2,100]{2,0,1:T(8,128)S(1)} all-to-all(f32[16,2,100]{2,0,1:T(8,128)S(1)} %copy.52), channel_id=1, replica_groups=mesh['rows'=16,'feat'=2] {'feat'}, dimensions={1} | all-to-all | bytes 25600 | tf_op jit(solution)/shard_map/all_to_all | solution.py:84
  128.4 19.0 %gather_fusion.2 = f32[3200]{0:T(1024)S(1)} fusion(f32[32,100]{1,0:T(8,128)S(1)} %bitcast.48, s32[3200]{0:T(1024)S(1)} %get-tuple-element.58), kind=kCustom, calls=%fused_computation.2 | custom fusion | bytes 51200 | tf_op jit(solution)/shard_map/gather | solution.py:100
  (75 shorter events, 24.5 us)
Async XLA Ops:
  3.4 38.2 %collective-permute-start = (bf16[1,64,128]{1,2,0:T(8,128)(2,1)S(1)}, bf16[1,64,128]{1,2,0:T(8,128)(2,1)S(1)}, u32[]{:S(2)}, u32[]{:S(2)}) collective-permute-start(bf16[1,64,128]{1,2,0:T(8,128)(2,1)S(1)} %bitcast.57), channel_id=1, source_target_pairs={{0,2},{2,0},{4,6},{6,4},{8,10},{10,8},{12,14},{14,12},{16,18},{18,... | collective-permute-start | bytes 49160 | tf_op jit(solution)/shard_map/ppermute | solution.py:18
  8.8 11.0 %copy-start.2 = (s32[2]{0:T(128)S(1)}, s32[2]{0:T(128)}, u32[]{:S(2)}) copy-start(s32[2]{0:T(128)} %constant.70) | copy-start | bytes 28
  8.8 11.1 %copy-start.1 = (s32[2]{0:T(128)S(1)}, s32[2]{0:T(128)}, u32[]{:S(2)}) copy-start(s32[2]{0:T(128)} %constant.67) | copy-start | bytes 28
  20.6 20.9 %copy-start = (s32[1024]{0:T(1024)S(1)}, s32[1024]{0:T(1024)}, u32[]{:S(2)}) copy-start(s32[1024]{0:T(1024)} %param.9) | copy-start | bytes 12292
  35.6 13.3 %all-to-all-start.2 = ((s32[16,2,200]{2,1,0:T(2,128)}), s32[16,2,200]{2,1,0:T(2,128)S(1)}, u32[]{:S(2)}, u32[]{:S(2)}) async-start(s32[16,2,200]{2,1,0:T(2,128)} %reshape.234), calls=%async_computation.2 | async-start | bytes 65536 | tf_op jit(solution)/shard_map/all_to_all | solution.py:64
  41.7 15.7 %collective-permute-start.1 = (bf16[2,64,128]{1,2,0:T(8,128)(2,1)S(1)}, bf16[2,64,128]{1,2,0:T(8,128)(2,1)S(1)}, u32[]{:S(2)}, u32[]{:S(2)}) collective-permute-start(bf16[2,64,128]{1,2,0:T(8,128)(2,1)S(1)} %get-tuple-element.64), channel_id=1, source_target_pairs={{0,4},{2,6},{4,0},{6,2},{8,12},{10,14},{12,8},{14,10},{16,20},{18,... | collective-permute-start | bytes 98312 | tf_op jit(solution)/shard_map/ppermute | solution.py:18
  57.5 5.6 %collective-permute-start.2 = (bf16[4,64,128]{1,2,0:T(8,128)(2,1)S(1)}, bf16[4,64,128]{1,2,0:T(8,128)(2,1)S(1)}, u32[]{:S(2)}, u32[]{:S(2)}) collective-permute-start(bf16[4,64,128]{1,2,0:T(8,128)(2,1)S(1)} %bitcast.55), channel_id=1, source_target_pairs={{0,8},{2,10},{4,12},{6,14},{8,0},{10,2},{12,4},{14,6},{16,24},{18,... | collective-permute-start | bytes 196616 | tf_op jit(solution)/shard_map/ppermute | solution.py:18
  63.4 9.2 %collective-permute-start.3 = (bf16[8,64,128]{2,1,0:T(8,128)(2,1)S(1)}, bf16[8,64,128]{2,1,0:T(8,128)(2,1)S(1)}, u32[]{:S(2)}, u32[]{:S(2)}) collective-permute-start(bf16[8,64,128]{2,1,0:T(8,128)(2,1)S(1)} %bitcast.53), channel_id=1, source_target_pairs={{0,16},{2,18},{4,20},{6,22},{8,24},{10,26},{12,28},{14,30},{16,0},... | collective-permute-start | bytes 393224 | tf_op jit(solution)/shard_map/ppermute | solution.py:18
  98.9 11.1 %all-to-all-start = ((f32[16,2,32]{2,1,0:T(2,128)}), f32[16,2,32]{2,1,0:T(2,128)S(1)}, u32[]{:S(2)}, u32[]{:S(2)}) async-start(f32[16,2,32]{2,1,0:T(2,128)} %reshape.229), calls=%async_computation | async-start | bytes 32768 | tf_op jit(solution)/shard_map/all_to_all | solution.py:92
  113.8 10.8 %all-to-all-start.4 = ((f32[16,2,100]{2,1,0:T(2,128)}), f32[16,2,100]{2,1,0:T(2,128)S(1)}, u32[]{:S(2)}, u32[]{:S(2)}) async-start(f32[16,2,100]{2,1,0:T(2,128)} %reshape.236), calls=%async_computation.4 | async-start | bytes 32768 | tf_op jit(solution)/shard_map/all_to_all | solution.py:85
